TPU v7x, 64 devices: a 2x2x8 block of a 4x4x8 slice. The times are simulated.
64 devices in a mesh: dp: 8 (over x, y, core), ep: 8 (over z).
Axes of the slice: x: 2, y: 2, z: 8, core: 2. Of those that a mesh axis runs over, the one named last changes fastest.
The devices are a block of a 4x4x8 slice.
Arguments:
- x: bfloat16 [8, 8, 256, 2048], P('dp', 'ep'), parts along dimension 0
- expert: int32 [8, 8, 256, 2], P('dp', 'ep'), parts along dimension 0
- slot: int32 [8, 8, 256, 2], P('dp', 'ep'), parts along dimension 0
- gate: float32 [8, 8, 256, 2], P('dp', 'ep'), parts along dimension 0
- w_gate: bfloat16 [8, 2048, 5632], P('ep')
- w_up: bfloat16 [8, 2048, 5632], P('ep')
- w_down: bfloat16 [8, 5632, 2048], P('ep')
Outputs:
- y: bfloat16 [8, 8, 256, 2048], P('dp', 'ep'), parts along dimension 0
There are 8 independent parts. A program takes and returns all parts, laid end to end along the dimension named above; an argument that names none is the same for every part.
All inputs are finite; a program needn't handle non-finite values.
Results may differ from a plain program's by a relative error of at most 0.009.
Values are sent between devices in bfloat16 or wider.
A program may use at most 768 MiB of HBM per device.

v0:
```python
import jax
import jax.numpy as jnp
from jax import lax
from jax.sharding import NamedSharding, PartitionSpec as P


def einsum(form, a, b):
    return jnp.einsum(form, a.astype(jnp.float32), b.astype(jnp.float32))


def solution(mesh):
    def placed(v, *spec):
        return lax.with_sharding_constraint(v, NamedSharding(mesh, P(*spec)))

    def step(x, expert, slot, gate, w_gate, w_up, w_down):
        experts, (tokens, top) = w_gate.shape[0], expert.shape[2:]
        slots = 5 * tokens * top // (4 * experts)
        to_expert = jax.nn.one_hot(expert, experts, dtype=jnp.bfloat16)
        to_slot = jax.nn.one_hot(slot, slots, dtype=jnp.bfloat16)
        weighted = to_expert * gate[..., None].astype(jnp.bfloat16)
        dispatch = einsum("abtke,abtkc->abtec", to_expert, to_slot).astype(jnp.bfloat16)
        combine = einsum("abtke,abtkc->abtec", weighted, to_slot).astype(jnp.bfloat16)
        z = einsum("abtec,abtd->aebcd", dispatch, x).astype(jnp.bfloat16)
        z = placed(z, "dp", None, "ep", None, None)
        z = placed(z, "dp", "ep", None, None, None)
        h = jax.nn.silu(einsum("aebcd,edf->aebcf", z, w_gate))
        h = (h * einsum("aebcd,edf->aebcf", z, w_up)).astype(jnp.bfloat16)
        out = einsum("aebcf,efd->aebcd", h, w_down).astype(jnp.bfloat16)
        out = placed(out, "dp", "ep", None, None, None)
        out = placed(out, "dp", None, "ep", None, None)
        y = einsum("abtec,aebcd->abtd", combine, out)
        return y.astype(jnp.bfloat16)

    return step
```

profile of v0, /device:TPU:21, one launch (start us, length us, event | category | flops | bytes accessed | tf_op | source)
XLA Modules:
  0.0 218.0 jit_solution(8737143736636350481)
XLA Ops:
  0.0 0.0 copy-start
  0.0 0.9 copy.3
  0.9 0.8 copy.5
  1.7 1.8 fusion.39
  3.5 0.3 copy.9
  3.8 0.0 copy-done
  3.8 0.8 fusion.22
  4.7 71.7 %all-to-all.4 = bf16[1,8,1,1,80,2048]{5,4,3,2,0,1:T(8,128)(2,1)S(1)} all-to-all(bf16[1,8,1,1,80,2048]{5,4,3,2,0,1:T(8,128)(2,1)S(1)} %fusion.22), channel_id=1, replica_groups=mesh['dp'=8,'ep'=8] {'ep'}, dimensions={1} | all-to-all | bytes 5242880 | tf_op jit(solution)/sharding_constraint;jit(solution)/sharding_constraint | solution.py:13
  76.4 0.0 copy-start.2
  76.4 1.5 copy-done.2
  77.9 22.4 %fusion.4 = f32[8,80,5632]{2,1,0:T(8,128)} fusion(bf16[1,2048,5632]{2,1,0:T(8,128)(2,1)} %param.4, bf16[1,8,1,1,80,2048]{5,4,3,2,0,1:T(8,128)(2,1)S(1)} %all-to-all.4), kind=kOutput, calls=%fused_computation.4 | convolution fusion | flops 14763950080 | bytes 40108032 | tf_op jit(solution)/aebcd,edf->aebcf/dot_general | solution.py:8
  100.3 24.5 %fusion.12.clone.8 = bf16[8,80,5632]{2,1,0:T(8,128)(2,1)} fusion(bf16[1,2048,5632]{2,1,0:T(8,128)(2,1)} %param.5, f32[8,80,5632]{2,1,0:T(8,128)} %fusion.4, bf16[1,8,1,1,80,2048]{5,4,3,2,0,1:T(8,128)(2,1)} %copy-done.2), kind=kOutput, calls=%fused_computation.13.clone.clone.clone.clone.clone.clone.clone.1 | convolution fusion | flops 14785576960 | bytes 47316992 | tf_op jit(solution)/aebcd,edf->aebcf/dot_general | solution.py:8
  124.9 0.0 copy-start.3
  124.9 0.0 copy-start.1
  124.9 21.5 %fusion.23 = bf16[1,1,8,1,80,2048]{5,4,3,1,0,2:T(8,128)(2,1)} fusion(bf16[1,5632,2048]{2,1,0:T(8,128)(2,1)} %param.6, bf16[8,80,5632]{2,1,0:T(8,128)(2,1)} %fusion.12.clone.8), kind=kOutput, calls=%fused_computation.17 | convolution fusion | flops 14765260800 | bytes 32899072 | tf_op jit(solution)/aebcf,efd->aebcd/dot_general | solution.py:8
  146.4 4.6 %all-to-all-start.1 = ((bf16[1,1,8,1,80,2048]{5,4,3,1,0,2:T(8,128)(2,1)}), bf16[1,1,8,1,80,2048]{5,4,3,1,0,2:T(8,128)(2,1)}, u32[]{:S(2)}, u32[]{:S(2)}) async-start(bf16[1,1,8,1,80,2048]{5,4,3,1,0,2:T(8,128)(2,1)} %fusion.23), calls=%async_computation.1 | async-start | bytes 5242880 | tf_op jit(solution)/sharding_constraint;jit(solution)/sharding_constraint | solution.py:13
  151.0 0.0 copy-done.3
  151.0 0.1 copy.4
  151.1 2.2 %fusion.42 = bf16[256,8,80]{2,1,0:T(8,128)(2,1)S(1)} fusion(s32[256,2]{1,0:T(8,128)S(1)} %copy.5, s32[256,2]{1,0:T(8,128)S(1)} %copy.3, bf16[256,2]{1,0:T(8,128)(2,1)S(1)} %copy.4), kind=kOutput, calls=%fused_computation.28 | convolution fusion | flops 704512 | bytes 332800 | tf_op jit(solution)/abtke,abtkc->abtec/dot_general | solution.py:8
  153.3 0.3 copy.8
  153.7 60.6 %all-to-all-done.1 = bf16[1,1,8,1,80,2048]{5,4,3,1,0,2:T(8,128)(2,1)} async-done(((bf16[1,1,8,1,80,2048]{5,4,3,1,0,2:T(8,128)(2,1)}), bf16[1,1,8,1,80,2048]{5,4,3,1,0,2:T(8,128)(2,1)}, u32[]{:S(2)}, u32[]{:S(2)}) %all-to-all-start.1) | async-done | bytes 2621472 | tf_op jit(solution)/sharding_constraint;jit(solution)/sharding_constraint | solution.py:13
  214.3 3.7 %fusion.35 = bf16[1,1,256,2048]{3,2,1,0:T(8,128)(2,1)} fusion(bf16[1,1,8,1,80,2048]{5,4,3,1,0,2:T(8,128)(2,1)} %all-to-all-done.1, bf16[256,8,80]{0,2,1:T(8,128)(2,1)S(1)} %copy.8), kind=kOutput, calls=%fused_computation.23 | convolution fusion | flops 671612928 | bytes 3997696 | tf_op jit(solution)/abtec,aebcd->abtd/dot_general | solution.py:8
  218.0 0.0 copy-done.1
  (1 shorter events, 0.0 us)
Async XLA Ops:
  0.0 3.8 %copy-start = (bf16[1,1,256,2048]{3,2,1,0:T(8,128)(2,1)S(1)}, bf16[1,1,256,2048]{3,2,1,0:T(8,128)(2,1)}, u32[]{:S(2)}) copy-start(bf16[1,1,256,2048]{3,2,1,0:T(8,128)(2,1)} %param.3) | copy-start | bytes 3145732
  76.4 1.5 copy-start.2
  124.9 26.1 %copy-start.3 = (f32[1,1,256,2]{2,3,1,0:T(2,128)S(1)}, f32[1,1,256,2]{2,3,1,0:T(2,128)}, u32[]{:S(2)}) copy-start(f32[1,1,256,2]{2,3,1,0:T(2,128)} %param.1) | copy-start | bytes 6148
  124.9 93.1 %copy-start.1 = (bf16[1,1,256,2048]{3,2,1,0:T(8,128)(2,1)S(1)}, bf16[1,1,256,2048]{3,2,1,0:T(8,128)(2,1)}, u32[]{:S(2)}) copy-start(bf16[1,1,256,2048]{3,2,1,0:T(8,128)(2,1)} %param.3) | copy-start | bytes 3145732
  146.4 67.9 %all-to-all-start.1 = ((bf16[1,1,8,1,80,2048]{5,4,3,1,0,2:T(8,128)(2,1)}), bf16[1,1,8,1,80,2048]{5,4,3,1,0,2:T(8,128)(2,1)}, u32[]{:S(2)}, u32[]{:S(2)}) async-start(bf16[1,1,8,1,80,2048]{5,4,3,1,0,2:T(8,128)(2,1)} %fusion.23), calls=%async_computation.1 | async-start | bytes 5242880 | tf_op jit(solution)/sharding_constraint;jit(solution)/sharding_constraint | solution.py:13
where the time goes:
time: 218 us
  matrix products  77 us (35%)
  blocking collectives  71.7 us (33%)
  waiting for transfers between devices  60.6 us (28%)
  starting transfers between devices  4.59 us (2%)
  local copies, waits for them, and re-layouts  4.05 us (2%)
    dot_general x7, matrix products, einsum(): return jnp.einsum(form, a.astype(jnp.float32), b.astype(jnp.float32))  77 us
    another operation x1, blocking collectives, placed(): return lax.with_sharding_constraint(v, NamedSharding(mesh, P(*spec)))  71.7 us
    another operation x1, waiting for transfers between devices, placed(): return lax.with_sharding_constraint(v, NamedSharding(mesh, P(*spec)))  60.6 us
    another operation x1, starting transfers between devices, placed(): return lax.with_sharding_constraint(v, NamedSharding(mesh, P(*spec)))  4.59 us
  transfers between devices with their start and end apart: 1, of which 1 were waited for; matrix products, arithmetic and copies ran while one was open for 1% of the time, Pallas kernels for 0%

commit v1 on v0

v1 whole, which is shorter than its diff:
```python
import functools

import jax
import jax.numpy as jnp
from jax import lax
from jax.experimental import pallas as pl
from jax.experimental.pallas import tpu as pltpu
from jax.sharding import PartitionSpec as P

MESH = pl.DeviceIdType.MESH
FIRST_SHARE = 3, 5
FT = 512
NT = 256
GROUP = 2
G_SLOTS = 6
D_SLOTS = 4
BF16, F32 = jnp.bfloat16, jnp.float32


def dot(a, b):
    return jnp.dot(a, b, preferred_element_type=F32)


def kernel(
    n, slots, ra, rb,
    expert_ref, slot_ref, gate_ref, x_hbm, wg_hbm, wu_hbm, wd_hbm, y_hbm,
    x_ref, zs_a, zs_b, zr_a, zr_b, h_ref, os_a, os_b, or_a, or_b, acc, cmb_a, cmb_b, yb, g_buf, d_buf,
    x_sem, g_sem, d_sem, y_sem, zss_a, zrs_a, zss_b, zrs_b, oss_a, ors_a, oss_b, ors_b,
):
    me = lax.axis_index("ep")
    tokens, depth = x_ref.shape
    g_tiles, d_tiles = wg_hbm.shape[1] // FT, wd_hbm.shape[1] // NT
    messages, width = d_tiles // GROUP, GROUP * NT
    rows_a, rows_b = n * ra, n * rb

    def peer(d):
        return {"ep": lax.rem(me + d, n)}

    x_copy = pltpu.make_async_copy(x_hbm, x_ref, x_sem)
    x_copy.start()
    barrier = pltpu.get_barrier_semaphore()
    for d in range(1, n):
        pl.semaphore_signal(barrier, inc=1, device_id=peer(d), device_id_type=MESH)

    def g_copies(p):
        slot, tile = lax.rem(p, G_SLOTS), lax.rem(p, g_tiles)
        cols = pl.ds(pl.multiple_of(tile * FT, FT), FT)
        return [
            pltpu.make_async_copy(w.at[:, cols], g_buf.at[slot, i], g_sem.at[slot, i])
            for i, w in enumerate((wg_hbm, wu_hbm))
        ]

    def d_copy(p):
        slot, tile = lax.rem(p, D_SLOTS), lax.rem(p, d_tiles)
        cols = pl.ds(pl.multiple_of(tile * NT, NT), NT)
        return pltpu.make_async_copy(wd_hbm.at[:, cols], d_buf.at[slot], d_sem.at[slot])

    @pl.loop(0, G_SLOTS)
    def _(p):
        for c in g_copies(p):
            c.start()

    @pl.loop(0, D_SLOTS)
    def _(p):
        d_copy(p).start()

    rel = expert_ref[...] - me
    rel = jnp.where(rel < 0, rel + n, rel)
    slot = slot_ref[...]
    code_a = jnp.where(slot < ra, rel * ra + slot, -1)
    code_b = jnp.where((slot >= ra) & (slot < slots), rel * rb + slot - ra, -1)

    def picks(code, rows):
        row = lax.broadcasted_iota(jnp.int32, (rows, tokens), 0)
        return row == code[0:1, :], row == code[1:2, :]

    x_copy.wait()
    x = x_ref[...]
    for code, rows, r, zs, zr in (
        (code_a, rows_a, ra, zs_a, zr_a),
        (code_b, rows_b, rb, zs_b, zr_b),
    ):
        p0, p1 = picks(code, rows)
        z = dot((p0 | p1).astype(F32).astype(BF16), x).astype(BF16)
        zr[0:r, :] = z[0:r]
        zs[r:, :] = z[r:]

    pl.semaphore_wait(barrier, n - 1)

    far_first = sorted(range(1, n), key=lambda d: (-min(d, n - d), d))

    def z_copy(d, r, zs, zr, send, recv):
        rows = pl.ds(d * r, r)
        return pltpu.make_async_remote_copy(
            src_ref=zs.at[rows], dst_ref=zr.at[rows], send_sem=send.at[d], recv_sem=recv.at[d],
            device_id=peer(d), device_id_type=MESH,
        )

    z_a = [z_copy(d, ra, zs_a, zr_a, zss_a, zrs_a) for d in far_first]
    z_b = [z_copy(d, rb, zs_b, zr_b, zss_b, zrs_b) for d in far_first]
    for c in z_a + z_b:
        c.start()

    gate = gate_ref[...].astype(BF16).astype(F32)
    for code, rows, cmb in ((code_a, rows_a, cmb_a), (code_b, rows_b, cmb_b)):
        p0, p1 = picks(code, rows)
        w = jnp.where(p0, gate[0:1, :], jnp.where(p1, gate[1:2, :], 0.0))
        cmb[...] = w.T.astype(BF16)

    def up(zr, rows, start, stop, fresh):
        @pl.loop(0, g_tiles)
        def _(i):
            p = start + i
            slot, tile = lax.rem(p, G_SLOTS), lax.rem(p, g_tiles)

            @pl.when(p >= fresh)
            def _():
                for c in g_copies(p):
                    c.wait()

            z = zr[...]
            g, u = dot(z, g_buf[slot, 0]), dot(z, g_buf[slot, 1])
            h_ref[0:rows, pl.ds(pl.multiple_of(tile * FT, FT), FT)] = (jax.nn.silu(g) * u).astype(BF16)

            @pl.when(p + G_SLOTS < stop)
            def _():
                for c in g_copies(p + G_SLOTS):
                    c.start()

    def o_copy(m, d, r, os, orr, send, recv):
        rows = pl.ds(d * r, r)
        return pltpu.make_async_remote_copy(
            src_ref=os.at[m, rows], dst_ref=orr.at[m, rows], send_sem=send.at[m, d], recv_sem=recv.at[m, d],
            device_id=peer(n - d), device_id_type=MESH,
        )

    def down(rows, r, os, orr, send, recv, start, stop, fresh):
        @pl.loop(0, messages)
        def _(i):
            m = lax.rem(start // GROUP + i, messages)
            for j in range(GROUP):
                p = start + GROUP * i + j
                slot = lax.rem(p, D_SLOTS)

                @pl.when(p >= fresh)
                def _():
                    d_copy(p).wait()

                o = dot(h_ref[0:rows, :], d_buf[slot]).astype(BF16)
                orr[m, 0:r, j * NT : (j + 1) * NT] = o[0:r]
                os[m, r:, j * NT : (j + 1) * NT] = o[r:]

                @pl.when(p + D_SLOTS < stop)
                def _():
                    d_copy(p + D_SLOTS).start()

            for d in far_first:
                o_copy(m, d, r, os, orr, send, recv).start()

    for c in z_a:
        c.wait_recv()
    up(zr_a, rows_a, 0, g_tiles, 0)
    down(rows_a, ra, os_a, or_a, oss_a, ors_a, 0, d_tiles, 0)
    for c in z_b:
        c.wait_recv()
    up(zr_b, rows_b, g_tiles - G_SLOTS, 2 * g_tiles - G_SLOTS, g_tiles)
    down(rows_b, rb, os_b, or_b, oss_b, ors_b, d_tiles - D_SLOTS, 2 * d_tiles - D_SLOTS, d_tiles)

    @pl.loop(0, messages)
    def _(m):
        for d in far_first:
            o_copy(m, d, ra, os_a, or_a, oss_a, ors_a).wait_recv()
        acc[m] = dot(cmb_a[...], or_a[m])

    def y_copy(m):
        cols = pl.ds(pl.multiple_of(m * width, width), width)
        return pltpu.make_async_copy(yb.at[m], y_hbm.at[:, cols], y_sem.at[m])

    @pl.loop(0, messages)
    def _(i):
        m = lax.rem((d_tiles - D_SLOTS) // GROUP + i, messages)
        for d in far_first:
            o_copy(m, d, rb, os_b, or_b, oss_b, ors_b).wait_recv()
        yb[m] = (acc[m] + dot(cmb_b[...], or_b[m])).astype(BF16)
        y_copy(m).start()

    for c in z_a + z_b:
        c.wait_send()

    @pl.loop(0, messages)
    def _(m):
        for d in far_first:
            o_copy(m, d, ra, os_a, or_a, oss_a, ors_a).wait_send()
            o_copy(m, d, rb, os_b, or_b, oss_b, ors_b).wait_send()
        y_copy(m).wait()


def solution(mesh):
    n = mesh.shape["ep"]

    def step(x, expert, slot, gate, w_gate, w_up, w_down):
        tokens, depth = x.shape[2:]
        top, hidden = expert.shape[3], w_gate.shape[2]
        slots = 5 * tokens * top // (4 * n)
        ra = slots * FIRST_SHARE[0] // FIRST_SHARE[1]
        rb = slots - ra
        messages, width = depth // (GROUP * NT), GROUP * NT
        vmem, any_space = pl.BlockSpec(memory_space=pltpu.VMEM), pl.BlockSpec(memory_space=pl.ANY)
        dma = pltpu.SemaphoreType.DMA
        y = pl.pallas_call(
            functools.partial(kernel, n, slots, ra, rb),
            out_shape=jax.ShapeDtypeStruct((tokens, depth), BF16),
            in_specs=[vmem] * 3 + [any_space] * 4,
            out_specs=any_space,
            scratch_shapes=[
                pltpu.VMEM((tokens, depth), BF16),
                pltpu.VMEM((n * ra, depth), BF16),
                pltpu.VMEM((n * rb, depth), BF16),
                pltpu.VMEM((n * ra, depth), BF16),
                pltpu.VMEM((n * rb, depth), BF16),
                pltpu.VMEM((n * max(ra, rb), hidden), BF16),
                pltpu.VMEM((messages, n * ra, width), BF16),
                pltpu.VMEM((messages, n * rb, width), BF16),
                pltpu.VMEM((messages, n * ra, width), BF16),
                pltpu.VMEM((messages, n * rb, width), BF16),
                pltpu.VMEM((messages, tokens, width), F32),
                pltpu.VMEM((tokens, n * ra), BF16),
                pltpu.VMEM((tokens, n * rb), BF16),
                pltpu.VMEM((messages, tokens, width), BF16),
                pltpu.VMEM((G_SLOTS, 2, depth, FT), BF16),
                pltpu.VMEM((D_SLOTS, hidden, NT), BF16),
                dma,
                dma((G_SLOTS, 2)),
                dma((D_SLOTS,)),
                dma((messages,)),
                dma((n,)),
                dma((n,)),
                dma((n,)),
                dma((n,)),
                dma((messages, n)),
                dma((messages, n)),
                dma((messages, n)),
                dma((messages, n)),
            ],
            compiler_params=pltpu.CompilerParams(
                collective_id=0, has_side_effects=True, vmem_limit_bytes=67_043_328
            ),
            name="moe",
        )(expert[0, 0].T, slot[0, 0].T, gate[0, 0].T, x[0, 0], w_gate[0], w_up[0], w_down[0])
        return y[None, None]

    tokens_spec, weights_spec = P("dp", "ep"), P("ep")
    return jax.shard_map(
        step,
        mesh=mesh,
        in_specs=(tokens_spec,) * 4 + (weights_spec,) * 3,
        out_specs=tokens_spec,
        check_vma=False,
    )
```

time: 218 us -> 132 us (0.61)
  Pallas kernels: 0 us -> 129 us
  matrix products: 77 us -> 0 us
  blocking collectives: 71.7 us -> 0 us
  waiting for transfers between devices: 60.6 us -> 0 us
  starting transfers between devices: 4.59 us -> 0 us
    pallas_call x0 -> x1, Pallas kernels: none -> 129 us  [step(): pl.pallas_call(functools.partial(kernel, n, slots, ra, rb), out_shape=jax...]
    dot_general x7 -> x0, matrix products: 77 us -> none  [einsum(): return jnp.einsum(form, a.astype(jnp.float32), b.astype(jnp.float32))]
    another operation x1 -> x0, blocking collectives: 71.7 us -> none  [placed(): return lax.with_sharding_constraint(v, NamedSharding(mesh, P(*spec)))]
    another operation x1 -> x0, waiting for transfers between devices: 60.6 us -> none  [placed(): return lax.with_sharding_constraint(v, NamedSharding(mesh, P(*spec)))]
    another operation x1 -> x0, starting transfers between devices: 4.59 us -> none  [placed(): return lax.with_sharding_constraint(v, NamedSharding(mesh, P(*spec)))]
  transfers between devices with their start and end apart: 1 -> 0, of which waited for: 1 -> 0; matrix products, arithmetic and copies ran while one was open for 1% -> 0% of each run, Pallas kernels for 0% -> 0%
where the time goes in v1:
time: 132 us; the launch traced here: 131 us
  Pallas kernels  129 us (98%)
  local copies, waits for them, and re-layouts  2.3 us (2%)
    pallas_call x1, Pallas kernels, step(): pl.pallas_call(functools.partial(kernel, n, slots, ra, rb), out_shape=jax...  129 us

profile of v1, /device:TPU:21, one launch (start us, length us, event | category | flops | bytes accessed | tf_op | source)
XLA Modules:
  0.0 130.8 jit_solution(12828281528211756778)
XLA Ops:
  0.0 128.5 %moe.1 = bf16[256,2048]{1,0:T(8,128)(2,1)} custom-call(s32[2,256]{1,0:T(2,128)} %bitcast.19, s32[2,256]{1,0:T(2,128)} %bitcast.20, f32[2,256]{1,0:T(2,128)} %bitcast.21, bf16[256,2048]{1,0:T(8,128)(2,1)} %bitcast.18, bf16[2048,5632]{1,0:T(8,128)(2,1)} %bitcast.14, bf16[2048,5632]{1,0:T(8,128)(2,1)} %bitcast.15, bf16[5632,2048]{1,0:T(8,128)(2,1)} %bitcast.16), custom_call_target="tpu_custom_call" | custom-call | tf_op jit(solution)/shard_map/moe/pallas_call | solution.py:210
  128.5 2.3 %copy.9 = bf16[1,1,256,2048]{3,2,1,0:T(8,128)(2,1)} copy(bf16[1,1,256,2048]{3,2,1,0:T(8,128)(2,1)} %bitcast.17) | data formatting | bytes 2097152
